TPU v7x, 32 devices: a whole 2x2x4 slice. The times are simulated.
32 devices in a mesh: dp: 16 (over z, y, x), tensor: 2 (over core).
Axes of the slice: x: 2, y: 2, z: 4, core: 2. Of those that a mesh axis runs over, the one named last changes fastest.
Arguments:
- inputs: bfloat16 [4, 8192, 768], P(None, ('dp', 'tensor')), may hold values from -6 to 6
- lengths: int32 [4, 16], P(None, 'dp'), may hold values from 128 to 512, as said below
- bounds: int32 [4, 16], P(None, 'dp'), may hold values from 32 to 384, as said below
- query_matrix: bfloat16 [768, 768], P('dp', 'tensor'), may hold values from -0.21875 to 0.21875
- key_matrix: bfloat16 [768, 768], P('dp', 'tensor'), may hold values from -0.21875 to 0.21875
- value_matrix: bfloat16 [768, 768], P('dp', 'tensor'), may hold values from -0.21875 to 0.21875
- query_value_bias: float32 [2, 768], P(None, 'tensor'), may hold values from -3 to 3
- adapter_down_weight: bfloat16 [2, 768, 8], P(None, 'dp'), may hold values from -0.21875 to 0.21875
- adapter_up_weight: bfloat16 [2, 8, 768], P(None, None, 'tensor'), may hold values from -1 to 1
- attention_output_weight: bfloat16 [768, 768], P('tensor', 'dp'), may hold values from -1.75 to 1.75
- feedforward_input_weight: bfloat16 [768, 3072], P('dp', 'tensor'), may hold values from -0.21875 to 0.21875
- feedforward_input_bias: float32 [3072], P('tensor'), may hold values from -3 to 3
- feedforward_output_weight: bfloat16 [3072, 768], P('tensor', 'dp'), may hold values from -0.109375 to 0.109375
- output_bias: float32 [2, 768], replicated, may hold values from -3 to 3
- layernorm_scale: float32 [2, 768], replicated, may hold values from 0.5 to 1.5
- layernorm_bias: float32 [2, 768], replicated, may hold values from -2 to 2
- output_gradient: bfloat16 [4, 8192, 768], P(None, ('dp', 'tensor')), may hold values from -6 to 6
Outputs:
- outputs: bfloat16 [4, 8192, 768], P(None, ('dp', 'tensor'))
- input_grad: float32 [4, 8192, 768], P(None, ('dp', 'tensor'))
- lora_up_grad: float32 [2, 8, 768], P(None, None, 'tensor')
Inputs may be any that keep to these rules, and one draw needn't show every extreme that they name: Item i of micro-batch m has live positions 0 to lengths[m, i] - 1 of its 512; the others are padding. An item's first segment is positions 0 to bounds - 1, its second bounds to 511; bounds lies between lengths // 4 and 3 * lengths // 4.
All inputs are finite; a program needn't handle non-finite values.
Results may differ from a plain program's by a relative error of at most 0.015.
The roundings to bfloat16 on the way count: a program that leaves them out, or rounds other values in their place, can miss the bound.
Values may be sent and summed in bfloat16 or wider, within the bound.
No kernel may reach another device: no remote copies, remote signals or barrier semaphores. Data moves between devices by JAX's collectives and lax.ppermute only.
A program may use at most 192 MiB of HBM per device.

v0:
```python
import jax
import jax.numpy as jnp
from jax import lax
from jax.sharding import PartitionSpec as P

HEAD_DIM = 64
UPDATE_RANK = 8
SLOT = 512
adapter_scale = 2.0
masked_value = -1000000000.0
norm_eps = 1e-05
highest_precision = lax.Precision.HIGHEST


def layer_norm(value_rows, gain, shift):
    centre = value_rows - jnp.mean(value_rows, axis=-1, keepdims=True)
    spread = jnp.mean(centre * centre, axis=-1, keepdims=True)
    return centre * lax.rsqrt(spread + norm_eps) * gain + shift


def exact_gelu(value_rows):
    return jax.nn.gelu(value_rows, approximate=False)


def item_mask(length, bound):
    places = jnp.arange(SLOT)
    segment = places >= bound
    return (places < length)[None, :] & (segment[:, None] == segment[None, :])


def split_heads(input_array):
    return input_array.reshape(input_array.shape[0], input_array.shape[1] // HEAD_DIM, HEAD_DIM)


def item_scores(query_heads, key_heads, length, bound):
    scores = (
        jnp.einsum("qhd,khd->hqk", query_heads, key_heads, preferred_element_type=jnp.float32)
        * 0.125
    )
    return jnp.where(item_mask(length, bound)[None], scores, masked_value)


def attend_forward(pieces):
    query_rows, keys, value_rows, length, bound = pieces
    query_heads = split_heads(query_rows)
    value_heads = split_heads(value_rows)
    scores = item_scores(query_heads, split_heads(keys), length, bound)
    peak = jnp.max(scores, axis=-1, keepdims=True)
    totals = jnp.log(jnp.sum(jnp.exp(scores - peak), axis=-1, keepdims=True)) + peak
    soft_weights = jnp.exp(scores - totals).astype(jnp.bfloat16)
    mixed = jnp.einsum(
        "hqk,khd->qhd", soft_weights, value_heads, preferred_element_type=jnp.float32
    )
    return (mixed.reshape(SLOT, query_rows.shape[1]).astype(jnp.bfloat16), totals)


def attend_backward(pieces):
    query_rows, keys, value_rows, grad_mixed, totals, length, bound = pieces
    query_heads = split_heads(query_rows)
    key_heads = split_heads(keys)
    grad_heads = split_heads(grad_mixed)
    scores = item_scores(query_heads, key_heads, length, bound)
    probs = jnp.exp(scores - totals)
    value_gradient = jnp.einsum(
        "hqk,qhd->khd", probs.astype(jnp.bfloat16), grad_heads, preferred_element_type=jnp.float32
    )
    grad_probs = jnp.einsum(
        "qhd,khd->hqk", grad_heads, split_heads(value_rows), preferred_element_type=jnp.float32
    )
    inner = jnp.sum(probs * grad_probs, axis=-1, keepdims=True)
    grad_scores = (probs * (grad_probs - inner)).astype(jnp.bfloat16)
    query_gradient = (
        jnp.einsum("hqk,khd->qhd", grad_scores, key_heads, preferred_element_type=jnp.float32)
        * 0.125
    )
    key_gradient = (
        jnp.einsum("hqk,qhd->khd", grad_scores, query_heads, preferred_element_type=jnp.float32)
        * 0.125
    )
    width = query_rows.shape[1]
    return (
        query_gradient.reshape(SLOT, width).astype(jnp.bfloat16),
        key_gradient.reshape(SLOT, width).astype(jnp.bfloat16),
        value_gradient.reshape(SLOT, width).astype(jnp.bfloat16),
    )


def contract_trailing(left, right):
    return lax.dot_general(
        left, right, (((1,), (1,)), ((), ())), preferred_element_type=jnp.float32
    )


def project_row_batch(
    input_rows,
    query_projected,
    key_projected,
    value_projected,
    down_projected,
    query_value_bias,
    adapter_up_weight,
):
    up_weight_float = adapter_up_weight.astype(jnp.float32)
    lowrank_update = jnp.einsum(
        "td,zdr->ztr", input_rows, down_projected, preferred_element_type=jnp.float32
    )
    query_rows = (
        jnp.dot(input_rows, query_projected, preferred_element_type=jnp.float32)
        + query_value_bias[0]
        + adapter_scale
        * jnp.dot(lowrank_update[0], up_weight_float[0], precision=highest_precision)
    ).astype(jnp.bfloat16)
    keys = jnp.dot(input_rows, key_projected, preferred_element_type=jnp.float32).astype(
        jnp.bfloat16
    )
    value_rows = (
        jnp.dot(input_rows, value_projected, preferred_element_type=jnp.float32)
        + query_value_bias[1]
        + adapter_scale
        * jnp.dot(lowrank_update[1], up_weight_float[1], precision=highest_precision)
    ).astype(jnp.bfloat16)
    return (lowrank_update, query_rows, keys, value_rows)


def adapter_components(lowrank_update, query_gradient, value_gradient):
    first_dims = (((0,), (0,)), ((), ()))
    return adapter_scale * jnp.stack(
        [
            lax.dot_general(
                lowrank_update[0],
                query_gradient.astype(jnp.float32),
                first_dims,
                precision=highest_precision,
            ),
            lax.dot_general(
                lowrank_update[1],
                value_gradient.astype(jnp.float32),
                first_dims,
                precision=highest_precision,
            ),
        ]
    )


def input_terms_all(
    query_gradient,
    key_gradient,
    value_gradient,
    query_projected,
    key_projected,
    value_projected,
    down_projected,
    adapter_up_weight,
):
    query_lowrank_gradient = adapter_scale * contract_trailing(query_gradient, adapter_up_weight[0])
    value_lowrank_gradient = adapter_scale * contract_trailing(value_gradient, adapter_up_weight[1])
    down_float = down_projected.astype(jnp.float32)
    total = contract_trailing(query_gradient, query_projected)
    total = total + contract_trailing(key_gradient, key_projected)
    total = total + contract_trailing(value_gradient, value_projected)
    total = total + lax.dot_general(
        query_lowrank_gradient, down_float[0], (((1,), (1,)), ((), ())), precision=highest_precision
    )
    total = total + lax.dot_general(
        value_lowrank_gradient, down_float[1], (((1,), (1,)), ((), ())), precision=highest_precision
    )
    return total


def forward_pass(rows_local, item_lengths, item_bounds, gathered, parameters):
    (
        query_projected,
        key_projected,
        value_projected,
        down_projected,
        out_full,
        ffn_in_full,
        ffn_out_full,
    ) = gathered
    (
        query_value_bias,
        adapter_up_weight,
        feedforward_input_bias,
        output_bias,
        layernorm_scale,
        layernorm_bias,
    ) = parameters
    group_items = item_lengths.shape[0]
    row_groups = lax.all_gather(rows_local, "tensor", axis=0, tiled=True)
    lowrank_update, query_rows, keys, value_rows = project_row_batch(
        row_groups,
        query_projected,
        key_projected,
        value_projected,
        down_projected,
        query_value_bias,
        adapter_up_weight,
    )
    width = query_rows.shape[1]
    item_shape = (group_items, SLOT, width)
    mixed, totals = lax.map(
        attend_forward,
        (
            query_rows.reshape(item_shape),
            keys.reshape(item_shape),
            value_rows.reshape(item_shape),
            item_lengths,
            item_bounds,
        ),
    )
    mixed_rows = mixed.reshape(group_items * SLOT, width)
    attended = lax.psum_scatter(
        jnp.dot(mixed_rows, out_full, preferred_element_type=jnp.float32),
        "tensor",
        scatter_dimension=0,
        tiled=True,
    )
    hidden_sum = rows_local.astype(jnp.float32) + attended + output_bias[0]
    normed = layer_norm(hidden_sum, layernorm_scale[0], layernorm_bias[0])
    pre_act = (
        jnp.dot(
            lax.all_gather(normed.astype(jnp.bfloat16), "tensor", axis=0, tiled=True),
            ffn_in_full,
            preferred_element_type=jnp.float32,
        )
        + feedforward_input_bias
    )
    activated = exact_gelu(pre_act).astype(jnp.bfloat16)
    ffn_total = (
        normed
        + lax.psum_scatter(
            jnp.dot(activated, ffn_out_full, preferred_element_type=jnp.float32),
            "tensor",
            scatter_dimension=0,
            tiled=True,
        )
        + output_bias[1]
    )
    result = layer_norm(ffn_total, layernorm_scale[1], layernorm_bias[1]).astype(jnp.bfloat16)
    kept = (lowrank_update, query_rows, keys, value_rows, totals, hidden_sum, pre_act, ffn_total)
    return (result, kept)


def layer_backward(grad_out, item_lengths, item_bounds, gathered, parameters, kept):
    (
        query_projected,
        key_projected,
        value_projected,
        down_projected,
        out_full,
        ffn_in_full,
        ffn_out_full,
    ) = gathered
    (
        query_value_bias,
        adapter_up_weight,
        feedforward_input_bias,
        output_bias,
        layernorm_scale,
        layernorm_bias,
    ) = parameters
    lowrank_update, query_rows, keys, value_rows, totals, hidden_sum, pre_act, ffn_total = kept
    group_items = item_lengths.shape[0]
    outer_pull = jax.vjp(
        lambda field: layer_norm(field, layernorm_scale[1], layernorm_bias[1]), ffn_total
    )[1]
    grad_sum = outer_pull(grad_out.astype(jnp.float32))[0]
    grad_act = contract_trailing(
        lax.all_gather(grad_sum.astype(jnp.bfloat16), "tensor", axis=0, tiled=True), ffn_out_full
    )
    gelu_pull = jax.vjp(exact_gelu, pre_act)[1]
    grad_pre = gelu_pull(grad_act)[0].astype(jnp.bfloat16)
    grad_normed = grad_sum + lax.psum_scatter(
        contract_trailing(grad_pre, ffn_in_full), "tensor", scatter_dimension=0, tiled=True
    )
    inner_pull = jax.vjp(
        lambda field: layer_norm(field, layernorm_scale[0], layernorm_bias[0]), hidden_sum
    )[1]
    grad_hidden = inner_pull(grad_normed)[0]
    grad_mixed = contract_trailing(
        lax.all_gather(grad_hidden.astype(jnp.bfloat16), "tensor", axis=0, tiled=True), out_full
    ).astype(jnp.bfloat16)
    width = query_rows.shape[1]
    item_shape = (group_items, SLOT, width)
    query_gradient, key_gradient, value_gradient = lax.map(
        attend_backward,
        (
            query_rows.reshape(item_shape),
            keys.reshape(item_shape),
            value_rows.reshape(item_shape),
            grad_mixed.reshape(item_shape),
            totals,
            item_lengths,
            item_bounds,
        ),
    )
    query_gradient = query_gradient.reshape(group_items * SLOT, width)
    key_gradient = key_gradient.reshape(group_items * SLOT, width)
    value_gradient = value_gradient.reshape(group_items * SLOT, width)
    adapter_portion = adapter_components(lowrank_update, query_gradient, value_gradient)
    row_gradient = grad_hidden + lax.psum_scatter(
        input_terms_all(
            query_gradient,
            key_gradient,
            value_gradient,
            query_projected,
            key_projected,
            value_projected,
            down_projected,
            adapter_up_weight,
        ).astype(jnp.bfloat16),
        "tensor",
        scatter_dimension=0,
        tiled=True,
    ).astype(jnp.float32)
    return (row_gradient, adapter_portion)


def local(
    inputs,
    lengths,
    bounds,
    query_matrix,
    key_matrix,
    value_matrix,
    query_value_bias,
    adapter_down_weight,
    adapter_up_weight,
    attention_output_weight,
    feedforward_input_weight,
    feedforward_input_bias,
    feedforward_output_weight,
    output_bias,
    layernorm_scale,
    layernorm_bias,
    output_gradient,
):
    micro_count = inputs.shape[0]
    parameters = (
        query_value_bias,
        adapter_up_weight,
        feedforward_input_bias,
        output_bias,
        layernorm_scale,
        layernorm_bias,
    )
    result_list = []
    gradient_tree = []
    adapter_combined = jnp.zeros((2, UPDATE_RANK, adapter_up_weight.shape[2]), jnp.float32)
    for batch_index in range(micro_count):
        forward_set = (
            lax.all_gather(query_matrix, "dp", axis=0, tiled=True),
            lax.all_gather(key_matrix, "dp", axis=0, tiled=True),
            lax.all_gather(value_matrix, "dp", axis=0, tiled=True),
            lax.all_gather(adapter_down_weight, "dp", axis=1, tiled=True),
            lax.all_gather(attention_output_weight, "dp", axis=1, tiled=True),
            lax.all_gather(feedforward_input_weight, "dp", axis=0, tiled=True),
            lax.all_gather(feedforward_output_weight, "dp", axis=1, tiled=True),
        )
        result, kept = forward_pass(
            inputs[batch_index], lengths[batch_index], bounds[batch_index], forward_set, parameters
        )
        backward_set = (
            lax.all_gather(query_matrix, "dp", axis=0, tiled=True),
            lax.all_gather(key_matrix, "dp", axis=0, tiled=True),
            lax.all_gather(value_matrix, "dp", axis=0, tiled=True),
            lax.all_gather(adapter_down_weight, "dp", axis=1, tiled=True),
            lax.all_gather(attention_output_weight, "dp", axis=1, tiled=True),
            lax.all_gather(feedforward_input_weight, "dp", axis=0, tiled=True),
            lax.all_gather(feedforward_output_weight, "dp", axis=1, tiled=True),
        )
        row_gradient, adapter_portion = layer_backward(
            output_gradient[batch_index],
            lengths[batch_index],
            bounds[batch_index],
            backward_set,
            parameters,
            kept,
        )
        adapter_combined = adapter_combined + lax.psum(adapter_portion, "dp")
        result_list.append(result)
        gradient_tree.append(row_gradient)
    return (jnp.stack(result_list), jnp.stack(gradient_tree), adapter_combined)


def solution(mesh):
    return jax.shard_map(
        local,
        mesh=mesh,
        in_specs=(
            P(None, ("dp", "tensor"), None),
            P(None, "dp"),
            P(None, "dp"),
            P("dp", "tensor"),
            P("dp", "tensor"),
            P("dp", "tensor"),
            P(None, "tensor"),
            P(None, "dp", None),
            P(None, None, "tensor"),
            P("tensor", "dp"),
            P("dp", "tensor"),
            P("tensor"),
            P("tensor", "dp"),
            P(),
            P(),
            P(),
            P(None, ("dp", "tensor"), None),
        ),
        out_specs=(
            P(None, ("dp", "tensor"), None),
            P(None, ("dp", "tensor"), None),
            P(None, None, "tensor"),
        ),
        check_vma=False,
    )
```

profile of v0, /device:TPU:0, one launch (start us, length us, event | category | flops | bytes accessed | tf_op | source)
XLA Modules:
  0.0 771.6 jit_solution(13941130316083166364)
XLA Ops:
  12.5 44.5 %all_gather.48 = bf16[2,768,8]{2,0,1:T(2,128)(2,1)S(1)} all-gather(bf16[2,48,8]{2,0,1:T(2,128)(2,1)S(1)} %copy.57), channel_id=1, replica_groups=mesh['dp'=16,'tensor'=2] {'dp'}, dimensions={1}, use_global_device_ids=true | all-gather | bytes 26112 | tf_op jit(solution)/shard_map/all_gather | solution.py:355
  57.3 39.2 %all_gather.49 = bf16[768,384]{1,0:T(8,128)(2,1)S(1)} all-gather(bf16[48,384]{1,0:T(8,128)(2,1)} %param.20), channel_id=1, replica_groups=mesh['dp'=16,'tensor'=2] {'dp'}, dimensions={0}, use_global_device_ids=true | all-gather | bytes 626688 | tf_op jit(solution)/shard_map/all_gather | solution.py:352
  96.5 41.1 %all_gather.50 = bf16[768,384]{1,0:T(8,128)(2,1)S(1)} all-gather(bf16[48,384]{1,0:T(8,128)(2,1)} %param.21), channel_id=1, replica_groups=mesh['dp'=16,'tensor'=2] {'dp'}, dimensions={0}, use_global_device_ids=true | all-gather | bytes 626688 | tf_op jit(solution)/shard_map/all_gather | solution.py:353
  137.5 39.3 %all_gather.47 = bf16[768,384]{1,0:T(8,128)(2,1)S(1)} all-gather(bf16[48,384]{1,0:T(8,128)(2,1)} %param.22), channel_id=1, replica_groups=mesh['dp'=16,'tensor'=2] {'dp'}, dimensions={0}, use_global_device_ids=true | all-gather | bytes 626688 | tf_op jit(solution)/shard_map/all_gather | solution.py:354
  176.8 40.8 %all_gather.51 = bf16[384,768]{0,1:T(8,128)(2,1)S(1)} all-gather(bf16[384,48]{0,1:T(8,128)(2,1)} %param.26), channel_id=1, replica_groups=mesh['dp'=16,'tensor'=2] {'dp'}, dimensions={1}, use_global_device_ids=true | all-gather | bytes 626688 | tf_op jit(solution)/shard_map/all_gather | solution.py:356
  218.5 2.4 all-gather.1
  232.9 3.3 all-gather
  247.4 3.1 all-gather.3
  261.4 3.2 all-gather.2
  278.0 2.6 reduce-scatter.25.cloned.1.call-done
  280.6 4.3 fusion.188
  286.7 2.8 all_gather.60
  289.5 47.2 %all-gather.7.cloned.1.call-done = bf16[768,1536]{1,0:T(8,128)(2,1)} async-done(((bf16[48,1536]{1,0:T(8,128)(2,1)}), bf16[768,1536]{1,0:T(8,128)(2,1)}) %all-gather.7.cloned.1.call-update) | async-done | bytes 2359312 | tf_op jit(solution)/shard_map/all_gather | solution.py:357
  336.7 10.4 %fusion.11 = (f32[512,1536]{1,0:T(8,128)}, f32[512,1536]{1,0:T(8,128)}) fusion(f32[1536]{0:T(1024)S(1)} %copy-done.198, bf16[512,768]{1,0:T(8,128)(2,1)S(1)} %all_gather.60, bf16[768,1536]{1,0:T(8,128)(2,1)} %all-gather.7.cloned.1.call-done), kind=kOutput, calls=%fused_computation.39 | convolution fusion | flops 1257504768 | bytes 9443328 | tf_op jit(solution)/shard_map/dot_general | solution.py:221
  347.2 52.7 %all-gather.9.cloned.1.call-done = bf16[1536,768]{0,1:T(8,128)(2,1)} async-done(((bf16[1536,48]{0,1:T(8,128)(2,1)}), bf16[1536,768]{0,1:T(8,128)(2,1)}) %all-gather.9.cloned.1.call-update) | async-done | bytes 2359312 | tf_op jit(solution)/shard_map/all_gather | solution.py:358
  399.9 6.1 fusion.35
  406.1 2.4 all_gather.58
  408.4 9.7 %fusion.10 = (f32[512,1536]{1,0:T(8,128)S(1)}, f32[512,1536]{1,0:T(8,128)S(1)}) fusion(f32[1536]{0:T(1024)} %param.28, bf16[512,768]{1,0:T(8,128)(2,1)S(1)} %all_gather.58, bf16[768,1536]{1,0:T(8,128)(2,1)} %all-gather.7.cloned.1.call-done), kind=kOutput, calls=%fused_computation.38 | convolution fusion | flops 1257504768 | bytes 9443328 | tf_op jit(solution)/shard_map/dot_general | solution.py:221
  420.8 2.7 fusion.34
  423.5 2.4 all_gather.56
  425.9 9.5 %fusion.9 = (f32[512,1536]{1,0:T(8,128)S(1)}, f32[512,1536]{1,0:T(8,128)S(1)}) fusion(f32[1536]{0:T(1024)} %param.28, bf16[512,768]{1,0:T(8,128)(2,1)S(1)} %all_gather.56, bf16[768,1536]{1,0:T(8,128)(2,1)} %all-gather.7.cloned.1.call-done), kind=kOutput, calls=%fused_computation.37 | convolution fusion | flops 1257504768 | bytes 9443328 | tf_op jit(solution)/shard_map/dot_general | solution.py:221
  438.1 2.6 fusion.33
  442.4 5.9 reduce-scatter.23.cloned.1.call-done
  448.4 4.5 fusion.187
  452.9 2.4 all_gather.52
  455.2 8.1 %fusion.8 = (f32[512,1536]{1,0:T(8,128)S(1)}, f32[512,1536]{1,0:T(8,128)S(1)}) fusion(f32[1536]{0:T(1024)S(1)} %copy-done.199, bf16[512,768]{1,0:T(8,128)(2,1)S(1)} %all_gather.52, bf16[768,1536]{1,0:T(8,128)(2,1)S(1)} %copy-done.197), kind=kOutput, calls=%fused_computation.36 | convolution fusion | flops 1257504768 | bytes 9443328 | tf_op jit(solution)/shard_map/dot_general | solution.py:221
  466.0 2.6 fusion.32
  468.7 10.4 %reduce-scatter.19.cloned.1.call-done = f32[256,768]{1,0:T(8,128)} async-done(((f32[512,768]{1,0:T(8,128)}), f32[256,768]{1,0:T(8,128)}) %reduce-scatter.19.cloned.1.call-update) | async-done | bytes 786448 | tf_op jit(solution)/shard_map/reduce_scatter | solution.py:231
  481.0 3.5 fusion.79
  486.7 2.5 all_gather.67
  489.2 7.8 %fusion.43 = f32[512,768]{1,0:T(8,128)} fusion(bf16[768,1536]{1,0:T(8,128)(2,1)} %all-gather.7.cloned.1.call-done, f32[512,1536]{1,0:T(8,128)} %get-tuple-element.339, f32[512,1536]{1,0:T(8,128)} %get-tuple-element.340, bf16[512,768]{1,0:T(8,128)(2,1)} %all_gather.67, bf16[1536,768]{0,1:T(8,128)(2,1)S(1)} %copy-done.4), kind=kOutput, calls=%fused_computation.117 | convolution fusion | flops 2426929152 | bytes 13369344 | tf_op jit(solution)/shard_map/dot_general | solution.py:89
  499.1 4.4 fusion.181
  504.5 2.5 all_gather.65
  507.1 7.8 %fusion.42 = f32[512,768]{1,0:T(8,128)} fusion(bf16[768,1536]{1,0:T(8,128)(2,1)} %all-gather.7.cloned.1.call-done, f32[512,1536]{1,0:T(8,128)} %copy-done.82, f32[512,1536]{1,0:T(8,128)} %copy-done.83, bf16[512,768]{1,0:T(8,128)(2,1)} %all_gather.65, bf16[1536,768]{0,1:T(8,128)(2,1)S(1)} %copy-done.4), kind=kOutput, calls=%fused_computation.116 | convolution fusion | flops 2426929152 | bytes 13369344 | tf_op jit(solution)/shard_map/dot_general | solution.py:89
  516.2 2.9 all_gather.61
  519.1 8.3 %fusion.40 = f32[512,768]{1,0:T(8,128)} fusion(bf16[768,1536]{1,0:T(8,128)(2,1)} %all-gather.7.cloned.1.call-done, f32[512,1536]{1,0:T(8,128)} %copy-done.84, f32[512,1536]{1,0:T(8,128)} %copy-done.85, bf16[512,768]{1,0:T(8,128)(2,1)} %all_gather.61, bf16[1536,768]{0,1:T(8,128)(2,1)S(1)} %copy-done.4), kind=kOutput, calls=%fused_computation.114 | convolution fusion | flops 2426929152 | bytes 13369344 | tf_op jit(solution)/shard_map/dot_general | solution.py:89
  528.8 2.5 all_gather.63
  531.3 7.8 %fusion.41 = f32[512,768]{1,0:T(8,128)} fusion(bf16[768,1536]{1,0:T(8,128)(2,1)} %all-gather.7.cloned.1.call-done, f32[512,1536]{1,0:T(8,128)} %copy-done.80, f32[512,1536]{1,0:T(8,128)} %copy-done.81, bf16[512,768]{1,0:T(8,128)(2,1)} %all_gather.63, bf16[1536,768]{0,1:T(8,128)(2,1)S(1)} %copy-done.4), kind=kOutput, calls=%fused_computation.115 | convolution fusion | flops 2426929152 | bytes 13369344 | tf_op jit(solution)/shard_map/dot_general | solution.py:89
  539.2 2.7 pad_maximum_fusion.1
  542.1 3.1 multiply_reduce_fusion.7
  545.2 5.8 reduce-scatter.37.cloned.1.call-done
  551.0 2.5 fusion.179
  553.7 2.5 all_gather.62
  556.9 4.6 convolution_convert_fusion.6
  564.5 2.5 all_gather.64
  572.1 2.4 all_gather.66
  580.7 2.5 all_gather.68
  588.9 4.6 multiply_reduce_fusion.3
  593.6 6.5 multiply_convert_fusion.3
  603.3 4.8 multiply_reduce_fusion.2
  608.2 4.7 multiply_reduce_fusion.1
  612.8 5.6 multiply_reduce_fusion
  622.1 6.7 multiply_convert_fusion.2
  630.5 4.9 multiply_convert_fusion.1
  637.3 4.7 multiply_convert_fusion
  647.8 2.1 add_convert_fusion.6
  650.3 2.2 convolution_bitcast_fusion.6
  657.6 2.1 add_convert_fusion.5
  659.8 2.1 convolution_bitcast_fusion.8
  667.1 2.1 add_convert_fusion.4
  676.5 77.1 %psum.34 = f32[2,8,384]{2,1,0:T(8,128)} all-reduce(f32[2,8,384]{2,1,0:T(8,128)S(1)} %fusion.110), channel_id=1, replica_groups=mesh['dp'=16,'tensor'=2] {'dp'}, use_global_device_ids=true, to_apply=%region_60.61 | all-reduce | flops 6144 | bytes 49152 | tf_op jit(solution)/shard_map/psum | solution.py:380
  755.6 2.1 add_bitcast_fusion.2
  757.7 2.1 add_bitcast_fusion.1
  761.0 3.1 pad_maximum_fusion
  (638 shorter events, 130.8 us)
Async XLA Ops:
  8.0 270.0 %reduce-scatter.21.cloned.1.call-start = ((), (), s32[]{:S(2)}) async-start(), calls=%async_computation.20 | async-start | bytes 2359296 | tf_op jit(solution)/shard_map/reduce_scatter | solution.py:212
  57.3 207.3 %copy-start.88 = (bf16[2,768,8]{1,2,0:T(8,128)(2,1)}, bf16[2,768,8]{1,2,0:T(8,128)(2,1)S(1)}, u32[]{:S(2)}) copy-start(bf16[2,768,8]{1,2,0:T(8,128)(2,1)S(1)} %copy.58) | copy-start | bytes 73732
  57.3 160.3 %copy-start.53 = (bf16[4,256,768]{2,1,0:T(8,128)(2,1)S(1)}, bf16[4,256,768]{2,1,0:T(8,128)(2,1)}, u32[]{:S(2)}) copy-start(bf16[4,256,768]{2,1,0:T(8,128)(2,1)} %param.17) | copy-start | bytes 4718596
  96.5 168.4 %copy-start.19 = (bf16[768,384]{1,0:T(8,128)(2,1)}, bf16[768,384]{1,0:T(8,128)(2,1)S(1)}, u32[]{:S(2)}) copy-start(bf16[768,384]{1,0:T(8,128)(2,1)S(1)} %all_gather.49) | copy-start | bytes 1769476
  137.5 129.9 %copy-start.14 = (bf16[768,384]{1,0:T(8,128)(2,1)}, bf16[768,384]{1,0:T(8,128)(2,1)S(1)}, u32[]{:S(2)}) copy-start(bf16[768,384]{1,0:T(8,128)(2,1)S(1)} %all_gather.50) | copy-start | bytes 1769476
  176.8 93.8 %copy-start.22 = (bf16[768,384]{1,0:T(8,128)(2,1)}, bf16[768,384]{1,0:T(8,128)(2,1)S(1)}, u32[]{:S(2)}) copy-start(bf16[768,384]{1,0:T(8,128)(2,1)S(1)} %all_gather.47) | copy-start | bytes 1769476
  217.6 56.1 %copy-start.24 = (bf16[384,768]{0,1:T(8,128)(2,1)}, bf16[384,768]{0,1:T(8,128)(2,1)S(1)}, u32[]{:S(2)}) copy-start(bf16[384,768]{0,1:T(8,128)(2,1)S(1)} %all_gather.51) | copy-start | bytes 1769476
  232.9 45.1 %reduce-scatter.17.cloned.1.call-start = ((), (), s32[]{:S(2)}) async-start(), calls=%async_computation.16 | async-start | bytes 2359296 | tf_op jit(solution)/shard_map/reduce_scatter | solution.py:212
  247.3 30.7 %reduce-scatter.29.cloned.1.call-start = ((), (), s32[]{:S(2)}) async-start(), calls=%async_computation.24 | async-start | bytes 2359296 | tf_op jit(solution)/shard_map/reduce_scatter | solution.py:212
  261.3 19.3 %reduce-scatter.25.cloned.1.call-start = ((), (), s32[]{:S(2)}) async-start(), calls=%async_computation.22 | async-start | bytes 2359296 | tf_op jit(solution)/shard_map/reduce_scatter | solution.py:212
  275.5 61.2 %all-gather.7.cloned.1.call-start = ((), (), s32[]{:S(2)}) async-start(), calls=%async_computation.17 | async-start | bytes 2506752 | tf_op jit(solution)/shard_map/all_gather | solution.py:357
  276.1 123.8 %all-gather.9.cloned.1.call-start = ((), (), s32[]{:S(2)}) async-start(), calls=%async_computation.18 | async-start | bytes 2506752 | tf_op jit(solution)/shard_map/all_gather | solution.py:358
  276.7 165.7 %reduce-scatter.31.cloned.1.call-start = ((), (), s32[]{:S(2)}) async-start(), calls=%async_computation.25 | async-start | bytes 2359296 | tf_op jit(solution)/shard_map/reduce_scatter | solution.py:231
  285.1 51.6 %copy-start.198 = (f32[1536]{0:T(1024)S(1)}, f32[1536]{0:T(1024)}, u32[]{:S(2)}) copy-start(f32[1536]{0:T(1024)} %param.28) | copy-start | bytes 18436
  406.0 36.4 %reduce-scatter.27.cloned.1.call-start = ((), (), s32[]{:S(2)}) async-start(), calls=%async_computation.23 | async-start | bytes 2359296 | tf_op jit(solution)/shard_map/reduce_scatter | solution.py:231
  408.4 12.3 %copy-start.4 = (bf16[1536,768]{0,1:T(8,128)(2,1)S(1)}, bf16[1536,768]{0,1:T(8,128)(2,1)}, u32[]{:S(2)}) copy-start(bf16[1536,768]{0,1:T(8,128)(2,1)} %all-gather.9.cloned.1.call-done) | copy-start | bytes 7077892
  423.4 24.9 %reduce-scatter.23.cloned.1.call-start = ((), (), s32[]{:S(2)}) async-start(), calls=%async_computation.21 | async-start | bytes 2359296 | tf_op jit(solution)/shard_map/reduce_scatter | solution.py:231
  438.1 10.2 %copy-start.142 = (f32[768]{0:T(1024)S(1)}, f32[768]{0:T(1024)}, u32[]{:S(2)}) copy-start(f32[768]{0:T(1024)} %get-tuple-element.175) | copy-start | bytes 9220
  438.1 10.2 %copy-start.144 = (f32[256]{0:T(256)S(1)}, f32[256]{0:T(256)}, u32[]{:S(2)}) copy-start(f32[256]{0:T(256)} %copy-done.143) | copy-start | bytes 3076
  438.1 10.2 %copy-start.148 = (f32[256]{0:T(256)S(1)}, f32[256]{0:T(256)}, u32[]{:S(2)}) copy-start(f32[256]{0:T(256)} %copy-done.147) | copy-start | bytes 3076
  438.1 10.2 %copy-start.152 = (f32[256]{0:T(256)S(1)}, f32[256]{0:T(256)}, u32[]{:S(2)}) copy-start(f32[256]{0:T(256)} %copy-done.151) | copy-start | bytes 3076
  438.1 10.2 %copy-start.165 = (f32[256]{0:T(256)S(1)}, f32[256]{0:T(256)}, u32[]{:S(2)}) copy-start(f32[256]{0:T(256)} %copy-done.164) | copy-start | bytes 3076
  438.1 10.2 %copy-start.168 = (f32[256]{0:T(256)S(1)}, f32[256]{0:T(256)}, u32[]{:S(2)}) copy-start(f32[256]{0:T(256)} %copy-done.167) | copy-start | bytes 3076
  438.1 10.2 %copy-start.171 = (f32[256]{0:T(256)S(1)}, f32[256]{0:T(256)}, u32[]{:S(2)}) copy-start(f32[256]{0:T(256)} %copy-done.170) | copy-start | bytes 3076
  440.7 38.3 %reduce-scatter.19.cloned.1.call-start = ((), (), s32[]{:S(2)}) async-start(), calls=%async_computation.19 | async-start | bytes 2359296 | tf_op jit(solution)/shard_map/reduce_scatter | solution.py:231
  442.3 10.6 %copy-start.189 = (f32[256]{0:T(256)}, f32[256]{0:T(256)S(1)}, u32[]{:S(2)}) copy-start(f32[256]{0:T(256)S(1)} %multiply_reduce_fusion.15) | copy-start | bytes 3076
  442.4 36.7 %copy-start.154 = (f32[256]{0:T(256)}, f32[256]{0:T(256)S(1)}, u32[]{:S(2)}) copy-start(f32[256]{0:T(256)S(1)} %fusion.147) | copy-start | bytes 3076
  448.4 6.9 copy-start.197
  448.4 6.9 copy-start.199
  468.6 73.4 %reduce-scatter.45.cloned.1.call-start = ((), (), s32[]{:S(2)}) async-start(), calls=%async_computation.32 | async-start | bytes 2359296 | tf_op jit(solution)/shard_map/reduce_scatter | solution.py:273
  468.6 15.8 %copy-start.179 = (f32[256]{0:T(256)}, f32[256]{0:T(256)S(1)}, u32[]{:S(2)}) copy-start(f32[256]{0:T(256)S(1)} %broadcast_multiply_fusion.4) | copy-start | bytes 3076
  468.6 15.8 %copy-start.180 = (f32[256]{0:T(256)}, f32[256]{0:T(256)S(1)}, u32[]{:S(2)}) copy-start(f32[256]{0:T(256)S(1)} %broadcast_multiply_fusion.2) | copy-start | bytes 3076
  468.7 15.8 %copy-start.182 = (f32[256]{0:T(256)}, f32[256]{0:T(256)S(1)}, u32[]{:S(2)}) copy-start(f32[256]{0:T(256)S(1)} %broadcast_multiply_fusion) | copy-start | bytes 3076
  489.2 10.0 %copy-start.141 = (f32[768]{0:T(1024)S(1)}, f32[768]{0:T(1024)}, u32[]{:S(2)}) copy-start(f32[768]{0:T(1024)} %get-tuple-element.173) | copy-start | bytes 9220
  497.0 45.0 %reduce-scatter.41.cloned.1.call-start = ((), (), s32[]{:S(2)}) async-start(), calls=%async_computation.30 | async-start | bytes 2359296 | tf_op jit(solution)/shard_map/reduce_scatter | solution.py:273
  503.5 11.4 %copy-start.158 = (f32[256]{0:T(256)}, f32[256]{0:T(256)S(1)}, u32[]{:S(2)}) copy-start(f32[256]{0:T(256)S(1)} %negate_multiply_fusion.7) | copy-start | bytes 3076
  507.1 7.9 %copy-start.196 = (f32[256]{0:T(256)S(1)}, f32[256]{0:T(256)}, u32[]{:S(2)}) copy-start(f32[256]{0:T(256)} %get-tuple-element.260) | copy-start | bytes 3076
  514.9 27.1 %reduce-scatter.33.cloned.1.call-start = ((), (), s32[]{:S(2)}) async-start(), calls=%async_computation.26 | async-start | bytes 2359296 | tf_op jit(solution)/shard_map/reduce_scatter | solution.py:273
  515.0 12.5 %copy-start.162 = (f32[256]{0:T(256)}, f32[256]{0:T(256)S(1)}, u32[]{:S(2)}) copy-start(f32[256]{0:T(256)S(1)} %negate_multiply_fusion.11) | copy-start | bytes 3076
  519.1 8.4 %copy-start.195 = (f32[256]{0:T(256)S(1)}, f32[256]{0:T(256)}, u32[]{:S(2)}) copy-start(f32[256]{0:T(256)} %get-tuple-element.194) | copy-start | bytes 3076
  527.5 23.6 %reduce-scatter.37.cloned.1.call-start = ((), (), s32[]{:S(2)}) async-start(), calls=%async_computation.28 | async-start | bytes 2359296 | tf_op jit(solution)/shard_map/reduce_scatter | solution.py:273
  539.1 214.4 %reduce-scatter.35.cloned.1.call-start = ((), (), s32[]{:S(2)}) async-start(), calls=%async_computation.27 | async-start | bytes 1179648 | tf_op jit(solution)/shard_map/reduce_scatter | solution.py:301
  541.9 9.1 %copy-start.153 = (f32[256]{0:T(256)S(1)}, f32[256]{0:T(256)}, u32[]{:S(2)}) copy-start(f32[256]{0:T(256)} %copy-done.151) | copy-start | bytes 3076
  541.9 9.1 %copy-start.155 = (f32[256]{0:T(256)S(1)}, f32[256]{0:T(256)}, u32[]{:S(2)}) copy-start(f32[256]{0:T(256)} %copy-done.154) | copy-start | bytes 3076
  541.9 9.1 %copy-start.161 = (f32[256]{0:T(256)S(1)}, f32[256]{0:T(256)}, u32[]{:S(2)}) copy-start(f32[256]{0:T(256)} %copy-done.160) | copy-start | bytes 3076
  541.9 9.1 %copy-start.163 = (f32[256]{0:T(256)S(1)}, f32[256]{0:T(256)}, u32[]{:S(2)}) copy-start(f32[256]{0:T(256)} %copy-done.162) | copy-start | bytes 3076
  556.9 10.7 %slice-start = ((s8[6291456]{0:T(1024)(128)(4,1)}), s8[4194304]{0:T(1024)(128)(4,1)S(1)}, s32[]{:S(2)}) async-start(s8[6291456]{0:T(1024)(128)(4,1)} %bitcast.410), calls=%async_computation.34 | async-start | bytes 8388608
  564.3 7.7 copy-start.34
  567.5 8.2 %slice-start.8 = ((s8[6291456]{0:T(1024)(128)(4,1)}), s8[4194304]{0:T(1024)(128)(4,1)S(1)}, s32[]{:S(2)}) async-start(s8[6291456]{0:T(1024)(128)(4,1)} %bitcast.418), calls=%async_computation.42 | async-start | bytes 8388608
  567.6 8.2 %slice-start.9 = ((s8[6291456]{0:T(1024)(128)(4,1)}), s8[2097152]{0:T(1024)(128)(4,1)S(1)}, s32[]{:S(2)}) async-start(s8[6291456]{0:T(1024)(128)(4,1)} %bitcast.418), calls=%async_computation.43 | async-start | bytes 4194304
  575.8 8.7 %slice-start.2 = ((s8[6291456]{0:T(1024)(128)(4,1)}), s8[4194304]{0:T(1024)(128)(4,1)S(1)}, s32[]{:S(2)}) async-start(s8[6291456]{0:T(1024)(128)(4,1)} %bitcast.412), calls=%async_computation.36 | async-start | bytes 8388608
  586.4 7.2 copy-start.75
  622.1 133.6 %reduce-scatter.39.cloned.1.call-start = ((), (), s32[]{:S(2)}) async-start(), calls=%async_computation.29 | async-start | bytes 1179648 | tf_op jit(solution)/shard_map/reduce_scatter | solution.py:301
  622.1 8.4 %slice-start.12 = ((s8[6291456]{0:T(1024)(128)(4,1)}), s8[4194304]{0:T(1024)(128)(4,1)S(1)}, s32[]{:S(2)}) async-start(s8[6291456]{0:T(1024)(128)(4,1)} %bitcast.422), calls=%async_computation.46 | async-start | bytes 8388608
  622.1 8.4 %slice-start.13 = ((s8[6291456]{0:T(1024)(128)(4,1)}), s8[2097152]{0:T(1024)(128)(4,1)S(1)}, s32[]{:S(2)}) async-start(s8[6291456]{0:T(1024)(128)(4,1)} %bitcast.422), calls=%async_computation.47 | async-start | bytes 4194304
  649.9 107.8 %reduce-scatter.43.cloned.1.call-start = ((), (), s32[]{:S(2)}) async-start(), calls=%async_computation.31 | async-start | bytes 1179648 | tf_op jit(solution)/shard_map/reduce_scatter | solution.py:301
  659.8 100.1 %reduce-scatter.47.cloned.1.call-start = ((), (), s32[]{:S(2)}) async-start(), calls=%async_computation.33 | async-start | bytes 1179648 | tf_op jit(solution)/shard_map/reduce_scatter | solution.py:301
  667.1 8.6 %copy-start.139 = (f32[1,8,384]{2,1,0:T(8,128)S(1)}, f32[1,8,384]{2,1,0:T(8,128)}, u32[]{:S(2)}) copy-start(f32[1,8,384]{2,1,0:T(8,128)} %convolution_bitcast_fusion.4) | copy-start | bytes 36868
  667.1 86.5 %copy-start.174 = (f32[256]{0:T(256)S(1)}, f32[256]{0:T(256)}, u32[]{:S(2)}) copy-start(f32[256]{0:T(256)} %copy-done.173) | copy-start | bytes 3076
  669.2 84.4 %copy-start.33 = (f32[256,768]{1,0:T(8,128)S(1)}, f32[256,768]{1,0:T(8,128)}, u32[]{:S(2)}) copy-start(f32[256,768]{1,0:T(8,128)} %copy-done.32) | copy-start | bytes 2359300
  669.2 86.4 %copy-start.37 = (f32[256,768]{1,0:T(8,128)S(1)}, f32[256,768]{1,0:T(8,128)}, u32[]{:S(2)}) copy-start(f32[256,768]{1,0:T(8,128)} %copy-done.36) | copy-start | bytes 2359300
  669.2 88.5 %copy-start.35 = (f32[256,768]{1,0:T(8,128)S(1)}, f32[256,768]{1,0:T(8,128)}, u32[]{:S(2)}) copy-start(f32[256,768]{1,0:T(8,128)} %copy-done.34) | copy-start | bytes 2359300
  674.2 85.6 %copy-start.40 = (f32[256,768]{1,0:T(8,128)S(1)}, f32[256,768]{1,0:T(8,128)}, u32[]{:S(2)}) copy-start(f32[256,768]{1,0:T(8,128)} %copy-done.39) | copy-start | bytes 2359300
  674.2 85.6 %copy-start.178 = (f32[256]{0:T(256)S(1)}, f32[256]{0:T(256)}, u32[]{:S(2)}) copy-start(f32[256]{0:T(256)} %copy-done.177) | copy-start | bytes 3076
  (168 other events, 570.6 us)
Sparse Core Ops, SparseCore 0:
  233.0 5.0 reduce-scatter.20
  247.4 5.1 reduce-scatter.16
  261.5 5.1 reduce-scatter.28
  275.6 4.9 reduce-scatter.24
  406.1 7.4 reduce-scatter.30
  423.6 7.4 reduce-scatter.26
  440.8 7.4 reduce-scatter.22
  468.7 10.3 reduce-scatter.18
  497.1 10.3 reduce-scatter.44
  515.0 10.3 reduce-scatter.40
  528.2 10.3 reduce-scatter.32
  540.7 10.3 reduce-scatter.36
  622.2 9.4 reduce-scatter.34
  650.1 9.4 reduce-scatter.38
  661.6 9.2 reduce-scatter.42
  673.6 9.2 reduce-scatter.46
Sparse Core Ops, SparseCore 1:
  278.8 57.9 all-gather.6
  339.4 60.4 all-gather.8
where the time goes:
time: 779 us; the launch traced here: 772 us
  blocking collectives  324 us (42%)
  matrix products  197 us (25%)
  waiting for transfers between devices  126 us (16%)
  other arithmetic  82.3 us (11%)
  local copies, waits for them, and re-layouts  22 us (3%)
  between operations  18.9 us (2%)
    psum x1, blocking collectives, local(): adapter_combined = adapter_combined + lax.psum(adapter_portion, 'dp')  77.1 us
    dot_general x28, matrix products, contract_trailing(): lax.dot_general(left, right, (((1,), (1,)), ((), ())), preferred_element_...  53.7 us
    all_gather x1, waiting for transfers between devices, local(): lax.all_gather(feedforward_output_weight, 'dp', axis=1, tiled=True)  52.7 us
    all_gather x1, waiting for transfers between devices, local(): lax.all_gather(feedforward_input_weight, 'dp', axis=0, tiled=True)  47.2 us
    all_gather x1, blocking collectives, local(): lax.all_gather(adapter_down_weight, 'dp', axis=1, tiled=True)  44.5 us
    all_gather x1, blocking collectives, local(): lax.all_gather(key_matrix, 'dp', axis=0, tiled=True)  41.1 us
    all_gather x1, blocking collectives, local(): lax.all_gather(attention_output_weight, 'dp', axis=1, tiled=True)  40.8 us
    all_gather x1, blocking collectives, local(): lax.all_gather(value_matrix, 'dp', axis=0, tiled=True)  39.3 us
  transfers between devices with their start and end apart: 18, of which 6 were waited for; matrix products, arithmetic and copies ran while one was open for 22% of the time, Pallas kernels for 0%

commit v1 on v0

--- a/solution.py
+++ b/solution.py
@@ -10,6 +10,28 @@
 masked_value = -1000000000.0
 norm_eps = 1e-05
 highest_precision = lax.Precision.HIGHEST
+
+
+def joined_along(parts, dim):
+    shape = list(parts.shape[1:])
+    shape[dim] *= parts.shape[0]
+    return jnp.moveaxis(parts, 0, dim).reshape(shape)
+
+
+def grow_blocks(shard, axis):
+    length = lax.axis_size(axis)
+    pieces = shard[None]
+    for level in range(length.bit_length() - 1):
+        bit = 1 << level
+        theirs = lax.ppermute(pieces, axis, [(i, i ^ bit) for i in range(length)])
+        both = jnp.stack([pieces, theirs])
+        upper = lax.axis_index(axis) >> level & 1
+        pieces = jnp.where(upper == 0, both, both[::-1]).reshape(-1, *shard.shape)
+    return pieces
+
+
+def gather_by_bits(array, axis, dim):
+    return joined_along(grow_blocks(array, axis), dim)
 
 
 def layer_norm(value_rows, gain, shift):
@@ -352,7 +374,7 @@
             lax.all_gather(query_matrix, "dp", axis=0, tiled=True),
             lax.all_gather(key_matrix, "dp", axis=0, tiled=True),
             lax.all_gather(value_matrix, "dp", axis=0, tiled=True),
-            lax.all_gather(adapter_down_weight, "dp", axis=1, tiled=True),
+            gather_by_bits(adapter_down_weight, "dp", 1),
             lax.all_gather(attention_output_weight, "dp", axis=1, tiled=True),
             lax.all_gather(feedforward_input_weight, "dp", axis=0, tiled=True),
             lax.all_gather(feedforward_output_weight, "dp", axis=1, tiled=True),

time: 779 us -> 805 us (1.033)
  matrix products: 197 us -> 211 us
    ppermute x0 -> x4, waiting for transfers between devices: none -> 9.39 us  [grow_blocks(): theirs = lax.ppermute(pieces, axis, [(i, i ^ bit) for i in range(length)])]
    unnamed x429 -> x449, local copies, waits for them, and re-layouts: 15.9 us -> 21.8 us
  transfers between devices with their start and end apart: 18 -> 22, of which waited for: 6 -> 8; matrix products, arithmetic and copies ran while one was open for 22% -> 25% of each run, Pallas kernels for 0% -> 0%
where the time goes in v1:
time: 805 us; the launch traced here: 795 us
  blocking collectives  318 us (40%)
  matrix products  211 us (26%)
  waiting for transfers between devices  132 us (16%)
  other arithmetic  81.9 us (10%)
  local copies, waits for them, and re-layouts  28.4 us (4%)
  between operations  19.1 us (2%)
    psum x1, blocking collectives, local(): adapter_combined = adapter_combined + lax.psum(adapter_portion, 'dp')  71.8 us
    dot_general x28, matrix products, contract_trailing(): lax.dot_general(left, right, (((1,), (1,)), ((), ())), preferred_element_...  53.7 us
    all_gather x1, waiting for transfers between devices, local(): lax.all_gather(feedforward_output_weight, 'dp', axis=1, tiled=True)  52.7 us
    all_gather x1, blocking collectives, local(): lax.all_gather(query_matrix, 'dp', axis=0, tiled=True)  43.7 us
    all_gather x1, blocking collectives, local(): lax.all_gather(adapter_down_weight, 'dp', axis=1, tiled=True)  43.4 us
    all_gather x1, waiting for transfers between devices, local(): lax.all_gather(feedforward_input_weight, 'dp', axis=0, tiled=True)  42.1 us
    all_gather x1, blocking collectives, local(): lax.all_gather(value_matrix, 'dp', axis=0, tiled=True)  41.2 us
    all_gather x1, blocking collectives, local(): lax.all_gather(key_matrix, 'dp', axis=0, tiled=True)  38.9 us
  transfers between devices with their start and end apart: 22, of which 8 were waited for; matrix products, arithmetic and copies ran while one was open for 25% of the time, Pallas kernels for 0%

profile of v1, /device:TPU:0, one launch (start us, length us, event | category | flops | bytes accessed | tf_op | source)
XLA Modules:
  0.0 795.1 jit_solution(6737066262286172848)
XLA Ops:
  8.0 3.0 collective-permute-start
  11.9 43.7 %all_gather.48 = bf16[768,384]{1,0:T(8,128)(2,1)S(1)} all-gather(bf16[48,384]{1,0:T(8,128)(2,1)} %param.20), channel_id=1, replica_groups=mesh['dp'=16,'tensor'=2] {'dp'}, dimensions={0}, use_global_device_ids=true | all-gather | bytes 626688 | tf_op jit(solution)/shard_map/all_gather | solution.py:374
  55.6 38.9 %all_gather.49 = bf16[768,384]{1,0:T(8,128)(2,1)S(1)} all-gather(bf16[48,384]{1,0:T(8,128)(2,1)} %param.21), channel_id=1, replica_groups=mesh['dp'=16,'tensor'=2] {'dp'}, dimensions={0}, use_global_device_ids=true | all-gather | bytes 626688 | tf_op jit(solution)/shard_map/all_gather | solution.py:375
  96.2 2.4 all-gather.3
  98.5 2.4 all-gather.2
  105.6 2.4 all-gather
  110.6 2.5 all-gather.1
  116.5 41.2 %all_gather.47 = bf16[768,384]{1,0:T(8,128)(2,1)S(1)} all-gather(bf16[48,384]{1,0:T(8,128)(2,1)S(1)} %copy-done.147), channel_id=1, replica_groups=mesh['dp'=16,'tensor'=2] {'dp'}, dimensions={0}, use_global_device_ids=true | all-gather | bytes 626688 | tf_op jit(solution)/shard_map/all_gather | solution.py:376
  157.7 38.8 %all_gather.50 = bf16[384,768]{0,1:T(8,128)(2,1)S(1)} all-gather(bf16[384,48]{0,1:T(8,128)(2,1)S(1)} %copy-done.148), channel_id=1, replica_groups=mesh['dp'=16,'tensor'=2] {'dp'}, dimensions={1}, use_global_device_ids=true | all-gather | bytes 626688 | tf_op jit(solution)/shard_map/all_gather | solution.py:378
  199.9 2.3 collective-permute-done.1
  202.7 3.5 collective-permute-done.2
  207.4 3.6 collective-permute-done.3
  229.3 2.4 fusion
  260.4 10.4 %reduce-scatter.25.cloned.1.call-done = f32[256,768]{1,0:T(8,128)} async-done(((f32[512,768]{1,0:T(8,128)}), f32[256,768]{1,0:T(8,128)}) %reduce-scatter.25.cloned.1.call-update) | async-done | bytes 786448 | tf_op jit(solution)/shard_map/reduce_scatter | solution.py:234
  270.8 3.7 fusion.198
  276.3 2.8 all_gather.59
  279.1 42.1 %all-gather.7.cloned.1.call-done = bf16[768,1536]{1,0:T(8,128)(2,1)} async-done(((bf16[48,1536]{1,0:T(8,128)(2,1)}), bf16[768,1536]{1,0:T(8,128)(2,1)}) %all-gather.7.cloned.1.call-update) | async-done | bytes 2359312 | tf_op jit(solution)/shard_map/all_gather | solution.py:379
  321.2 10.4 %fusion.11 = (f32[512,1536]{1,0:T(8,128)}, f32[512,1536]{1,0:T(8,128)}) fusion(f32[1536]{0:T(1024)S(1)} %copy-done.207, bf16[512,768]{1,0:T(8,128)(2,1)S(1)} %all_gather.59, bf16[768,1536]{1,0:T(8,128)(2,1)} %all-gather.7.cloned.1.call-done), kind=kOutput, calls=%fused_computation.39 | convolution fusion | flops 1257504768 | bytes 9443328 | tf_op jit(solution)/shard_map/dot_general | solution.py:243
  331.7 52.7 %all-gather.9.cloned.1.call-done = bf16[1536,768]{0,1:T(8,128)(2,1)} async-done(((bf16[1536,48]{0,1:T(8,128)(2,1)}), bf16[1536,768]{0,1:T(8,128)(2,1)}) %all-gather.9.cloned.1.call-update) | async-done | bytes 2359312 | tf_op jit(solution)/shard_map/all_gather | solution.py:380
  384.4 6.1 fusion.35
  390.5 2.4 all_gather.57
  392.9 9.7 %fusion.10 = (f32[512,1536]{1,0:T(8,128)S(1)}, f32[512,1536]{1,0:T(8,128)S(1)}) fusion(f32[1536]{0:T(1024)} %param.28, bf16[512,768]{1,0:T(8,128)(2,1)S(1)} %all_gather.57, bf16[768,1536]{1,0:T(8,128)(2,1)} %all-gather.7.cloned.1.call-done), kind=kOutput, calls=%fused_computation.38 | convolution fusion | flops 1257504768 | bytes 9443328 | tf_op jit(solution)/shard_map/dot_general | solution.py:243
  405.2 2.6 fusion.34
  407.9 2.4 all_gather.55
  410.2 9.5 %fusion.9 = (f32[512,1536]{1,0:T(8,128)S(1)}, f32[512,1536]{1,0:T(8,128)S(1)}) fusion(f32[1536]{0:T(1024)} %param.28, bf16[512,768]{1,0:T(8,128)(2,1)S(1)} %all_gather.55, bf16[768,1536]{1,0:T(8,128)(2,1)} %all-gather.7.cloned.1.call-done), kind=kOutput, calls=%fused_computation.37 | convolution fusion | flops 1257504768 | bytes 9443328 | tf_op jit(solution)/shard_map/dot_general | solution.py:243
  422.5 2.6 fusion.33
  426.8 5.9 reduce-scatter.23.cloned.1.call-done
  432.8 4.5 fusion.197
  437.3 2.4 all_gather.51
  439.6 8.1 %fusion.8 = (f32[512,1536]{1,0:T(8,128)S(1)}, f32[512,1536]{1,0:T(8,128)S(1)}) fusion(f32[1536]{0:T(1024)S(1)} %copy-done.208, bf16[512,768]{1,0:T(8,128)(2,1)S(1)} %all_gather.51, bf16[768,1536]{1,0:T(8,128)(2,1)S(1)} %copy-done.206), kind=kOutput, calls=%fused_computation.36 | convolution fusion | flops 1257504768 | bytes 9443328 | tf_op jit(solution)/shard_map/dot_general | solution.py:243
  450.4 2.6 fusion.32
  453.2 10.4 %reduce-scatter.19.cloned.1.call-done = f32[256,768]{1,0:T(8,128)} async-done(((f32[512,768]{1,0:T(8,128)}), f32[256,768]{1,0:T(8,128)}) %reduce-scatter.19.cloned.1.call-update) | async-done | bytes 786448 | tf_op jit(solution)/shard_map/reduce_scatter | solution.py:253
  465.4 3.4 fusion.79
  471.1 2.5 all_gather.67
  473.6 7.8 fusion.43
  483.6 4.3 fusion.191
  488.9 2.5 all_gather.65
  491.4 7.8 fusion.42
  500.6 2.9 all_gather.60
  503.5 8.3 %fusion.40 = f32[512,768]{1,0:T(8,128)} fusion(bf16[768,1536]{1,0:T(8,128)(2,1)} %all-gather.7.cloned.1.call-done, f32[512,1536]{1,0:T(8,128)} %copy-done.86, f32[512,1536]{1,0:T(8,128)} %copy-done.87, bf16[512,768]{1,0:T(8,128)(2,1)} %all_gather.60, bf16[1536,768]{0,1:T(8,128)(2,1)S(1)} %copy-done.4), kind=kOutput, calls=%fused_computation.114 | convolution fusion | flops 2426929152 | bytes 13369344 | tf_op jit(solution)/shard_map/dot_general | solution.py:111
  513.2 2.5 all_gather.63
  515.7 7.8 fusion.41
  525.1 43.4 %all_gather.62 = bf16[2,768,8]{2,0,1:T(2,128)(2,1)S(1)} all-gather(bf16[2,48,8]{2,0,1:T(2,128)(2,1)} %copy.63), channel_id=1, replica_groups=mesh['dp'=16,'tensor'=2] {'dp'}, dimensions={1}, use_global_device_ids=true | all-gather | bytes 26112 | tf_op jit(solution)/shard_map/all_gather | solution.py:389
  573.4 2.6 pad_maximum_fusion.1
  576.1 3.1 multiply_reduce_fusion.7
  579.3 2.5 fusion.189
  582.0 2.5 all_gather.61
  585.2 4.6 convolution_convert_fusion.6
  592.8 2.5 all_gather.64
  600.4 2.4 all_gather.66
  609.0 2.5 all_gather.136
  617.3 4.7 multiply_reduce_fusion.3
  621.9 6.5 multiply_convert_fusion.3
  631.7 4.8 multiply_reduce_fusion.2
  636.5 4.7 multiply_reduce_fusion.1
  641.2 5.6 multiply_reduce_fusion
  648.3 2.1 add_convert_fusion.7
  650.5 7.1 multiply_convert_fusion.2
  659.4 4.9 multiply_convert_fusion.1
  666.1 4.7 multiply_convert_fusion
  679.0 2.2 convolution_bitcast_fusion.6
  705.2 71.8 %psum.34 = f32[2,8,384]{2,1,0:T(8,128)} all-reduce(f32[2,8,384]{2,1,0:T(8,128)S(1)} %fusion.110), channel_id=1, replica_groups=mesh['dp'=16,'tensor'=2] {'dp'}, use_global_device_ids=true, to_apply=%region_60.61 | all-reduce | flops 6144 | bytes 49152 | tf_op jit(solution)/shard_map/psum | solution.py:402
  781.2 2.1 add_bitcast_fusion.1
  784.4 3.1 pad_maximum_fusion
  (676 shorter events, 157.7 us)
Async XLA Ops:
  8.0 252.4 %reduce-scatter.21.cloned.1.call-start = ((), (), s32[]{:S(2)}) async-start(), calls=%async_computation.20 | async-start | bytes 2359296 | tf_op jit(solution)/shard_map/reduce_scatter | solution.py:234
  8.0 190.5 %collective-permute-start = (bf16[1,2,48,8]{2,3,1,0:T(8,128)(2,1)}, bf16[1,2,48,8]{2,3,1,0:T(8,128)(2,1)S(1)}, u32[]{:S(2)}, u32[]{:S(2)}) collective-permute-start(bf16[1,2,48,8]{2,3,1,0:T(8,128)(2,1)} %bitcast.523), channel_id=1, source_target_pairs={{0,2},{2,0},{4,6},{6,4},{8,10},{10,8},{12,14},{14,12},{16,18},{18,... | collective-permute-start | bytes 4616 | tf_op jit(solution)/shard_map/ppermute | solution.py:26
  55.6 58.8 %copy-start.19 = (bf16[768,384]{1,0:T(8,128)(2,1)}, bf16[768,384]{1,0:T(8,128)(2,1)S(1)}, u32[]{:S(2)}) copy-start(bf16[768,384]{1,0:T(8,128)(2,1)S(1)} %all_gather.48) | copy-start | bytes 1769476
  94.5 18.6 %copy-start.14 = (bf16[768,384]{1,0:T(8,128)(2,1)}, bf16[768,384]{1,0:T(8,128)(2,1)S(1)}, u32[]{:S(2)}) copy-start(bf16[768,384]{1,0:T(8,128)(2,1)S(1)} %all_gather.49) | copy-start | bytes 1769476
  101.4 139.6 %copy-start.90 = (bf16[512,384]{0,1:T(8,128)(2,1)}, bf16[512,384]{0,1:T(8,128)(2,1)S(1)}, u32[]{:S(2)}) copy-start(bf16[512,384]{0,1:T(8,128)(2,1)S(1)} %convolution_convert_fusion.9) | copy-start | bytes 1179652
  110.6 47.0 %copy-start.148 = (bf16[384,48]{0,1:T(8,128)(2,1)S(1)}, bf16[384,48]{0,1:T(8,128)(2,1)}, u32[]{:S(2)}) copy-start(bf16[384,48]{0,1:T(8,128)(2,1)} %param.26) | copy-start | bytes 110596
  113.1 84.8 %copy-start.81 = (bf16[1,512,768]{2,1,0:T(8,128)(2,1)}, bf16[1,512,768]{2,1,0:T(8,128)(2,1)S(1)}, u32[]{:S(2)}) copy-start(bf16[1,512,768]{2,1,0:T(8,128)(2,1)S(1)} %all-gather.1) | copy-start | bytes 2359300
  114.4 83.5 %copy-start.199 = (s32[4,1]{0,1:T(1,128)S(1)}, s32[4,1]{0,1:T(1,128)}, u32[]{:S(2)}) copy-start(s32[4,1]{0,1:T(1,128)} %param.19) | copy-start | bytes 52
  114.4 84.1 %copy-start.162 = (bf16[2,48,8]{1,2,0:T(8,128)(2,1)S(1)}, bf16[2,48,8]{1,2,0:T(8,128)(2,1)}, u32[]{:S(2)}) copy-start(bf16[2,48,8]{1,2,0:T(8,128)(2,1)} %param.24) | copy-start | bytes 4612
  115.8 96.9 %copy-start.105 = (bf16[2,8,384]{2,1,0:T(8,128)(2,1)S(1)}, bf16[2,8,384]{2,1,0:T(8,128)(2,1)}, u32[]{:S(2)}) copy-start(bf16[2,8,384]{2,1,0:T(8,128)(2,1)} %param.25) | copy-start | bytes 36868
  157.7 91.3 %copy-start.22 = (bf16[768,384]{1,0:T(8,128)(2,1)}, bf16[768,384]{1,0:T(8,128)(2,1)S(1)}, u32[]{:S(2)}) copy-start(bf16[768,384]{1,0:T(8,128)(2,1)S(1)} %all_gather.47) | copy-start | bytes 1769476
  196.5 59.6 %copy-start.24 = (bf16[384,768]{0,1:T(8,128)(2,1)}, bf16[384,768]{0,1:T(8,128)(2,1)S(1)}, u32[]{:S(2)}) copy-start(bf16[384,768]{0,1:T(8,128)(2,1)S(1)} %all_gather.50) | copy-start | bytes 1769476
  198.6 3.7 collective-permute-start.1
  202.3 3.8 collective-permute-start.2
  202.7 16.2 %copy-start.41 = (pred[512,512]{0,1:T(8,128)(4,1)}, pred[512,512]{0,1:T(8,128)(4,1)S(1)}, u32[]{:S(2)}) copy-start(pred[512,512]{0,1:T(8,128)(4,1)S(1)} %compare_and_fusion.2) | copy-start | bytes 786436
  206.2 4.9 collective-permute-start.3
  223.7 36.7 %reduce-scatter.17.cloned.1.call-start = ((), (), s32[]{:S(2)}) async-start(), calls=%async_computation.16 | async-start | bytes 2359296 | tf_op jit(solution)/shard_map/reduce_scatter | solution.py:234
  238.0 22.4 %reduce-scatter.29.cloned.1.call-start = ((), (), s32[]{:S(2)}) async-start(), calls=%async_computation.24 | async-start | bytes 2359296 | tf_op jit(solution)/shard_map/reduce_scatter | solution.py:234
  248.4 22.4 %reduce-scatter.25.cloned.1.call-start = ((), (), s32[]{:S(2)}) async-start(), calls=%async_computation.22 | async-start | bytes 2359296 | tf_op jit(solution)/shard_map/reduce_scatter | solution.py:234
  256.1 14.7 %copy-start.53 = (bf16[4,256,768]{2,1,0:T(8,128)(2,1)S(1)}, bf16[4,256,768]{2,1,0:T(8,128)(2,1)}, u32[]{:S(2)}) copy-start(bf16[4,256,768]{2,1,0:T(8,128)(2,1)} %param.17) | copy-start | bytes 4718596
  257.9 63.3 %all-gather.7.cloned.1.call-start = ((), (), s32[]{:S(2)}) async-start(), calls=%async_computation.17 | async-start | bytes 2506752 | tf_op jit(solution)/shard_map/all_gather | solution.py:379
  258.5 125.9 %all-gather.9.cloned.1.call-start = ((), (), s32[]{:S(2)}) async-start(), calls=%async_computation.18 | async-start | bytes 2506752 | tf_op jit(solution)/shard_map/all_gather | solution.py:380
  259.1 167.7 %reduce-scatter.31.cloned.1.call-start = ((), (), s32[]{:S(2)}) async-start(), calls=%async_computation.25 | async-start | bytes 2359296 | tf_op jit(solution)/shard_map/reduce_scatter | solution.py:253
  274.8 46.4 %copy-start.207 = (f32[1536]{0:T(1024)S(1)}, f32[1536]{0:T(1024)}, u32[]{:S(2)}) copy-start(f32[1536]{0:T(1024)} %param.28) | copy-start | bytes 18436
  390.5 36.3 %reduce-scatter.27.cloned.1.call-start = ((), (), s32[]{:S(2)}) async-start(), calls=%async_computation.23 | async-start | bytes 2359296 | tf_op jit(solution)/shard_map/reduce_scatter | solution.py:253
  392.9 12.4 %copy-start.4 = (bf16[1536,768]{0,1:T(8,128)(2,1)S(1)}, bf16[1536,768]{0,1:T(8,128)(2,1)}, u32[]{:S(2)}) copy-start(bf16[1536,768]{0,1:T(8,128)(2,1)} %all-gather.9.cloned.1.call-done) | copy-start | bytes 7077892
  407.8 24.9 %reduce-scatter.23.cloned.1.call-start = ((), (), s32[]{:S(2)}) async-start(), calls=%async_computation.21 | async-start | bytes 2359296 | tf_op jit(solution)/shard_map/reduce_scatter | solution.py:253
  422.5 10.2 %copy-start.146 = (f32[768]{0:T(1024)S(1)}, f32[768]{0:T(1024)}, u32[]{:S(2)}) copy-start(f32[768]{0:T(1024)} %get-tuple-element.175) | copy-start | bytes 9220
  422.5 10.2 %copy-start.150 = (f32[256]{0:T(256)S(1)}, f32[256]{0:T(256)}, u32[]{:S(2)}) copy-start(f32[256]{0:T(256)} %copy-done.149) | copy-start | bytes 3076
  422.5 10.2 %copy-start.154 = (f32[256]{0:T(256)S(1)}, f32[256]{0:T(256)}, u32[]{:S(2)}) copy-start(f32[256]{0:T(256)} %copy-done.153) | copy-start | bytes 3076
  422.5 10.2 %copy-start.158 = (f32[256]{0:T(256)S(1)}, f32[256]{0:T(256)}, u32[]{:S(2)}) copy-start(f32[256]{0:T(256)} %copy-done.157) | copy-start | bytes 3076
  422.5 10.2 %copy-start.172 = (f32[256]{0:T(256)S(1)}, f32[256]{0:T(256)}, u32[]{:S(2)}) copy-start(f32[256]{0:T(256)} %copy-done.171) | copy-start | bytes 3076
  422.5 10.2 %copy-start.175 = (f32[256]{0:T(256)S(1)}, f32[256]{0:T(256)}, u32[]{:S(2)}) copy-start(f32[256]{0:T(256)} %copy-done.174) | copy-start | bytes 3076
  422.5 10.2 %copy-start.178 = (f32[256]{0:T(256)S(1)}, f32[256]{0:T(256)}, u32[]{:S(2)}) copy-start(f32[256]{0:T(256)} %copy-done.177) | copy-start | bytes 3076
  425.1 38.4 %reduce-scatter.19.cloned.1.call-start = ((), (), s32[]{:S(2)}) async-start(), calls=%async_computation.19 | async-start | bytes 2359296 | tf_op jit(solution)/shard_map/reduce_scatter | solution.py:253
  426.7 10.5 %copy-start.196 = (f32[256]{0:T(256)}, f32[256]{0:T(256)S(1)}, u32[]{:S(2)}) copy-start(f32[256]{0:T(256)S(1)} %multiply_reduce_fusion.15) | copy-start | bytes 3076
  426.8 36.8 %copy-start.160 = (f32[256]{0:T(256)}, f32[256]{0:T(256)S(1)}, u32[]{:S(2)}) copy-start(f32[256]{0:T(256)S(1)} %fusion.157) | copy-start | bytes 3076
  453.0 122.9 %reduce-scatter.45.cloned.1.call-start = ((), (), s32[]{:S(2)}) async-start(), calls=%async_computation.32 | async-start | bytes 2359296 | tf_op jit(solution)/shard_map/reduce_scatter | solution.py:295
  453.1 15.8 %copy-start.186 = (f32[256]{0:T(256)}, f32[256]{0:T(256)S(1)}, u32[]{:S(2)}) copy-start(f32[256]{0:T(256)S(1)} %broadcast_multiply_fusion.4) | copy-start | bytes 3076
  453.1 15.8 %copy-start.187 = (f32[256]{0:T(256)}, f32[256]{0:T(256)S(1)}, u32[]{:S(2)}) copy-start(f32[256]{0:T(256)S(1)} %broadcast_multiply_fusion.2) | copy-start | bytes 3076
  453.1 15.8 %copy-start.189 = (f32[256]{0:T(256)}, f32[256]{0:T(256)S(1)}, u32[]{:S(2)}) copy-start(f32[256]{0:T(256)S(1)} %broadcast_multiply_fusion) | copy-start | bytes 3076
  473.6 10.0 %copy-start.145 = (f32[768]{0:T(1024)S(1)}, f32[768]{0:T(1024)}, u32[]{:S(2)}) copy-start(f32[768]{0:T(1024)} %get-tuple-element.173) | copy-start | bytes 9220
  481.4 94.6 %reduce-scatter.41.cloned.1.call-start = ((), (), s32[]{:S(2)}) async-start(), calls=%async_computation.30 | async-start | bytes 2359296 | tf_op jit(solution)/shard_map/reduce_scatter | solution.py:295
  487.9 11.3 %copy-start.165 = (f32[256]{0:T(256)}, f32[256]{0:T(256)S(1)}, u32[]{:S(2)}) copy-start(f32[256]{0:T(256)S(1)} %negate_multiply_fusion.7) | copy-start | bytes 3076
  499.3 76.8 %reduce-scatter.33.cloned.1.call-start = ((), (), s32[]{:S(2)}) async-start(), calls=%async_computation.26 | async-start | bytes 2359296 | tf_op jit(solution)/shard_map/reduce_scatter | solution.py:295
  499.3 12.5 %copy-start.169 = (f32[256]{0:T(256)}, f32[256]{0:T(256)S(1)}, u32[]{:S(2)}) copy-start(f32[256]{0:T(256)S(1)} %negate_multiply_fusion.11) | copy-start | bytes 3076
  511.8 67.4 %reduce-scatter.37.cloned.1.call-start = ((), (), s32[]{:S(2)}) async-start(), calls=%async_computation.28 | async-start | bytes 2359296 | tf_op jit(solution)/shard_map/reduce_scatter | solution.py:295
  511.9 11.6 %copy-start.167 = (f32[256]{0:T(256)}, f32[256]{0:T(256)S(1)}, u32[]{:S(2)}) copy-start(f32[256]{0:T(256)S(1)} %negate_multiply_fusion.9) | copy-start | bytes 3076
  523.5 52.6 %copy-start.5 = (f32[256,768]{1,0:T(8,128)S(1)}, f32[256,768]{1,0:T(8,128)}, u32[]{:S(2)}) copy-start(f32[256,768]{1,0:T(8,128)} %get-tuple-element.269) | copy-start | bytes 2359300
  523.5 52.6 %copy-start.7 = (f32[256,768]{1,0:T(8,128)S(1)}, f32[256,768]{1,0:T(8,128)}, u32[]{:S(2)}) copy-start(f32[256,768]{1,0:T(8,128)} %copy-done.6) | copy-start | bytes 2359300
  523.5 52.6 %copy-start.9 = (f32[256,768]{1,0:T(8,128)S(1)}, f32[256,768]{1,0:T(8,128)}, u32[]{:S(2)}) copy-start(f32[256,768]{1,0:T(8,128)} %copy-done.8) | copy-start | bytes 2359300
  523.5 52.6 %copy-start.151 = (f32[256]{0:T(256)S(1)}, f32[256]{0:T(256)}, u32[]{:S(2)}) copy-start(f32[256]{0:T(256)} %copy-done.149) | copy-start | bytes 3076
  523.5 52.6 %copy-start.155 = (f32[256]{0:T(256)S(1)}, f32[256]{0:T(256)}, u32[]{:S(2)}) copy-start(f32[256]{0:T(256)} %copy-done.153) | copy-start | bytes 3076
  523.5 253.5 %reduce-scatter.35.cloned.1.call-start = ((), (), s32[]{:S(2)}) async-start(), calls=%async_computation.27 | async-start | bytes 1179648 | tf_op jit(solution)/shard_map/reduce_scatter | solution.py:323
  585.2 10.7 %slice-start = ((s8[6291456]{0:T(1024)(128)(4,1)}), s8[4194304]{0:T(1024)(128)(4,1)S(1)}, s32[]{:S(2)}) async-start(s8[6291456]{0:T(1024)(128)(4,1)} %bitcast.439), calls=%async_computation.34 | async-start | bytes 8388608
  650.5 128.6 %reduce-scatter.39.cloned.1.call-start = ((), (), s32[]{:S(2)}) async-start(), calls=%async_computation.29 | async-start | bytes 1179648 | tf_op jit(solution)/shard_map/reduce_scatter | solution.py:323
  678.7 102.4 %reduce-scatter.43.cloned.1.call-start = ((), (), s32[]{:S(2)}) async-start(), calls=%async_computation.31 | async-start | bytes 1179648 | tf_op jit(solution)/shard_map/reduce_scatter | solution.py:323
  688.5 94.7 %reduce-scatter.47.cloned.1.call-start = ((), (), s32[]{:S(2)}) async-start(), calls=%async_computation.33 | async-start | bytes 1179648 | tf_op jit(solution)/shard_map/reduce_scatter | solution.py:323
  695.9 81.1 %copy-start.181 = (f32[256]{0:T(256)S(1)}, f32[256]{0:T(256)}, u32[]{:S(2)}) copy-start(f32[256]{0:T(256)} %copy-done.180) | copy-start | bytes 3076
  697.9 79.1 %copy-start.33 = (f32[256,768]{1,0:T(8,128)S(1)}, f32[256,768]{1,0:T(8,128)}, u32[]{:S(2)}) copy-start(f32[256,768]{1,0:T(8,128)} %copy-done.32) | copy-start | bytes 2359300
  697.9 81.1 %copy-start.37 = (f32[256,768]{1,0:T(8,128)S(1)}, f32[256,768]{1,0:T(8,128)}, u32[]{:S(2)}) copy-start(f32[256,768]{1,0:T(8,128)} %copy-done.36) | copy-start | bytes 2359300
  698.0 83.2 %copy-start.35 = (f32[256,768]{1,0:T(8,128)S(1)}, f32[256,768]{1,0:T(8,128)}, u32[]{:S(2)}) copy-start(f32[256,768]{1,0:T(8,128)} %copy-done.34) | copy-start | bytes 2359300
  703.0 80.3 %copy-start.40 = (f32[256,768]{1,0:T(8,128)S(1)}, f32[256,768]{1,0:T(8,128)}, u32[]{:S(2)}) copy-start(f32[256,768]{1,0:T(8,128)} %copy-done.39) | copy-start | bytes 2359300
  703.0 80.3 %copy-start.185 = (f32[256]{0:T(256)S(1)}, f32[256]{0:T(256)}, u32[]{:S(2)}) copy-start(f32[256]{0:T(256)} %copy-done.184) | copy-start | bytes 3076
  (181 other events, 678.3 us)
Sparse Core Ops, SparseCore 0:
  223.8 7.2 reduce-scatter.20
  238.1 7.0 reduce-scatter.16
  248.5 9.1 reduce-scatter.28
  260.4 10.3 reduce-scatter.24
  390.6 7.4 reduce-scatter.30
  407.9 7.4 reduce-scatter.26
  425.2 7.4 reduce-scatter.22
  453.2 10.3 reduce-scatter.18
  481.6 10.3 reduce-scatter.44
  499.4 10.3 reduce-scatter.40
  512.6 10.3 reduce-scatter.32
  525.0 10.3 reduce-scatter.36
  650.6 4.0 reduce-scatter.34
  678.8 4.0 reduce-scatter.38
  688.6 5.7 reduce-scatter.42
  698.1 8.2 reduce-scatter.46
Sparse Core Ops, SparseCore 1:
  261.2 60.0 all-gather.6
  323.9 60.4 all-gather.8
